TPU v7x, 512 devices: a whole 4x8x8 slice. The times are simulated.
512 devices in a mesh: dp: 16 (over z, core), fsdp: 32 (over x, y).
Axes of the slice: x: 4, y: 8, z: 8, core: 2. Of those that a mesh axis runs over, the one named last changes fastest.
Arguments:
- replica_grads: bfloat16 [16, 8192, 4096], P('dp', 'fsdp'), may hold values from -4 to 4
- slot_table: int32 [32], replicated, may hold values from 0 to 63, as said below
- left_gram_state: float32 [64, 4, 16, 16, 1024], P('fsdp', None, 'dp')
- right_gram_state: float32 [64, 4, 16, 16, 1024], P('fsdp', None, 'dp')
- left_inverse_root: bfloat16 [64, 4, 16, 16, 1024], P('fsdp', None, 'dp')
- right_inverse_root: bfloat16 [64, 4, 16, 16, 1024], P('fsdp', None, 'dp')
Outputs:
- direction: bfloat16 [32, 16, 16, 4096], P('fsdp', 'dp')
- left_new: float32 [64, 4, 16, 16, 1024], P('fsdp', None, 'dp')
- right_new: float32 [64, 4, 16, 16, 1024], P('fsdp', None, 'dp')
Inputs may be any that keep to these rules, and one draw needn't show every extreme that they name: `slot_table`: the entries are distinct; slot v belongs to owner v // 2 of the flat shards' devices; some owner holds 2 blocks.
All inputs are finite; a program needn't handle non-finite values.
Results may differ from a plain program's by a relative error of at most 0.02.
Values may be sent and summed in bfloat16 or wider, within the bound.
No kernel may reach another device: no remote copies, remote signals or barrier semaphores. Data moves between devices by JAX's collectives and lax.ppermute only.
A program may use at most 128 MiB of HBM per device.

v0:
```python
import jax
import jax.numpy as jnp
from jax import lax
from jax.sharding import PartitionSpec as P


def on_device(
    replica_grads,
    slot_table,
    left_gram_state,
    right_gram_state,
    left_inverse_root,
    right_inverse_root,
):
    slots_here = left_gram_state.shape[0]
    sub_blocks = left_gram_state.shape[1]
    strip_rows = left_gram_state.shape[3]
    block_size = left_gram_state.shape[4]
    band_rows = replica_grads.shape[1]
    model_width = replica_grads.shape[2]
    per_band = model_width // block_size
    shards = lax.axis_size("fsdp")
    groups = lax.axis_size("dp")
    total_slots = shards * slots_here
    block_count = slot_table.shape[0]
    band_index = lax.axis_index("fsdp")
    strip_index = lax.axis_index("dp")
    slot_indices = jnp.arange(total_slots, dtype=jnp.int32)
    right_entire = lax.all_gather(right_inverse_root, "dp", axis=2, tiled=True).reshape(
        slots_here, block_size, block_size
    )
    summed = lax.psum_scatter(
        replica_grads[0].astype(jnp.float32).astype(jnp.bfloat16),
        "dp",
        scatter_dimension=0,
        tiled=True,
    )
    row_block = band_index * band_rows // block_size
    targets = lax.dynamic_slice_in_dim(slot_table, row_block * per_band, per_band, 0)
    chooser = (targets[:, None] == slot_indices[None, :]).astype(jnp.bfloat16)
    own_slots = band_index * slots_here + jnp.arange(slots_here, dtype=jnp.int32)
    holder = slot_table[None, :] == own_slots[:, None]
    block_of = jnp.sum(
        jnp.where(holder, jnp.arange(block_count, dtype=jnp.int32)[None, :], 0), axis=1
    )
    first_band = block_of // per_band * sub_blocks
    outgoing = jnp.einsum(
        "cn,tcb->ntb",
        chooser,
        summed.reshape(strip_rows, per_band, block_size),
        preferred_element_type=jnp.float32,
    ).astype(jnp.bfloat16)
    outgoing = outgoing.reshape(shards, slots_here, strip_rows, block_size)
    arrived = lax.all_to_all(outgoing, "fsdp", split_axis=0, concat_axis=0, tiled=True)
    owned_rows = jax.vmap(
        lambda portion, offset: lax.dynamic_slice_in_dim(portion, offset, sub_blocks, 0),
        in_axes=(1, 0),
    )(arrived, first_band)
    owned_rows = owned_rows.reshape(slots_here, sub_blocks, 1, strip_rows, block_size)
    entire = lax.all_gather(owned_rows, "dp", axis=2, tiled=True).reshape(
        slots_here, block_size, block_size
    )
    my_rows = owned_rows.reshape(slots_here, sub_blocks * strip_rows, block_size)
    left_gram = jnp.einsum("mrc,mnc->mrn", my_rows, entire, preferred_element_type=jnp.float32)
    left_new = left_gram_state + (left_gram / block_size).reshape(left_gram_state.shape)
    my_columns = lax.dynamic_index_in_dim(
        entire.reshape(slots_here, block_size, sub_blocks, groups, strip_rows),
        strip_index,
        3,
        keepdims=False,
    )
    my_columns = my_columns.reshape(slots_here, block_size, sub_blocks * strip_rows)
    right_gram = jnp.einsum("mnr,mnc->mrc", my_columns, entire, preferred_element_type=jnp.float32)
    right_new = right_gram_state + (right_gram / block_size).reshape(right_gram_state.shape)
    left_rows = left_inverse_root.reshape(slots_here, sub_blocks * strip_rows, block_size)
    mixed_rows = jnp.einsum(
        "mrn,mnc->mrc", left_rows, entire, preferred_element_type=jnp.float32
    ).astype(jnp.bfloat16)
    result = jnp.einsum(
        "mrn,mnc->mrc", mixed_rows, right_entire, preferred_element_type=jnp.float32
    )
    outcome = result.astype(jnp.bfloat16).reshape(slots_here, sub_blocks, strip_rows, block_size)
    homeward = jax.vmap(
        lambda portion, offset: lax.dynamic_update_slice_in_dim(
            jnp.zeros((shards, strip_rows, block_size), jnp.bfloat16), portion, offset, 0
        ),
        out_axes=1,
    )(outcome, first_band)
    returned = lax.all_to_all(homeward, "fsdp", split_axis=0, concat_axis=0, tiled=True)
    picked = jnp.einsum(
        "cn,ntb->tcb",
        chooser,
        returned.reshape(total_slots, strip_rows, block_size),
        preferred_element_type=jnp.float32,
    ).astype(jnp.bfloat16)
    direction = picked.reshape(1, 1, strip_rows, model_width)
    return (direction, left_new, right_new)


def solution(mesh):
    placed = (
        P("dp", "fsdp", None),
        P(),
        P("fsdp", None, "dp", None, None),
        P("fsdp", None, "dp", None, None),
        P("fsdp", None, "dp", None, None),
        P("fsdp", None, "dp", None, None),
    )
    return jax.shard_map(
        on_device,
        mesh=mesh,
        in_specs=placed,
        out_specs=(
            P("fsdp", "dp", None, None),
            P("fsdp", None, "dp", None, None),
            P("fsdp", None, "dp", None, None),
        ),
        check_vma=False,
    )
```

profile of v0, /device:TPU:16, one launch (start us, length us, event | category | flops | bytes accessed | tf_op | source)
XLA Modules:
  0.0 276.2 jit_solution(1561728517146626942)
XLA Ops:
  7.2 0.7 reduce-scatter.2.cloned.1.call-update
  8.0 0.7 all-gather.4.cloned.1.call-update
  8.7 0.7 dynamic_slice.7
  9.4 69.5 %reduce-scatter.2.cloned.1.call-done = bf16[16,4096]{1,0:T(8,128)(2,1)} async-done(((bf16[256,4096]{1,0:T(8,128)(2,1)}), bf16[16,4096]{1,0:T(8,128)(2,1)}) %reduce-scatter.2.cloned.1.call-update) | async-done | bytes 131088 | tf_op jit(solution)/shard_map/reduce_scatter | solution.py:32
  78.9 1.0 reshape.110
  79.9 0.8 convolution_convert_fusion
  80.7 2.5 copy.35
  83.2 9.8 %all-to-all-start = ((bf16[32,2,16,1024]{3,2,1,0:T(8,128)(2,1)}), bf16[32,2,16,1024]{3,2,1,0:T(8,128)(2,1)S(1)}, u32[]{:S(2)}, u32[]{:S(2)}) async-start(bf16[32,2,16,1024]{3,2,1,0:T(8,128)(2,1)} %bitcast.3), calls=%async_computation.1 | async-start | bytes 4194304 | tf_op jit(solution)/shard_map/all_to_all | solution.py:54
  93.3 45.8 %all-to-all-done = bf16[32,2,16,1024]{3,2,1,0:T(8,128)(2,1)S(1)} async-done(((bf16[32,2,16,1024]{3,2,1,0:T(8,128)(2,1)}), bf16[32,2,16,1024]{3,2,1,0:T(8,128)(2,1)S(1)}, u32[]{:S(2)}, u32[]{:S(2)}) %all-to-all-start) | async-done | bytes 2097184 | tf_op jit(solution)/shard_map/all_to_all | solution.py:54
  139.1 1.3 gather_fusion
  140.6 42.7 %all-gather.6.cloned.1.call-done = bf16[2,4,256,1024]{3,2,1,0:T(8,128)(2,1)} async-done(((bf16[2,4,16,1024]{3,2,1,0:T(8,128)(2,1)}), bf16[2,4,256,1024]{3,2,1,0:T(8,128)(2,1)}) %all-gather.6.cloned.1.call-update) | async-done | bytes 4194320 | tf_op jit(solution)/shard_map/all_gather | solution.py:60
  183.4 5.1 %convolution_convert_fusion.2 = bf16[2,64,1024]{2,1,0:T(8,128)(2,1)S(1)} fusion(bf16[2,1024,1024]{2,1,0:T(8,128)(2,1)} %bitcast.80, bf16[2,64,1024]{2,1,0:T(8,128)(2,1)S(1)} %bitcast.75, bf16[2,1024,1024]{2,1,0:T(8,128)(2,1)} %bitcast.76), kind=kOutput, calls=%fused_computation.12 | convolution fusion | flops 537133056 | bytes 8912896 | tf_op jit(solution)/shard_map/mrn,mnc->mrc/dot_general | solution.py:79
  188.4 1.6 broadcast_in_dim.16.clone
  190.0 17.4 %while.1 = (s32[]{:T(128)}, bf16[2,32,16,1024]{3,2,0,1:T(8,128)(2,1)}, s32[2,4]{1,0:T(2,128)S(1)}, bf16[2,4,16,1024]{3,2,1,0:T(8,128)(2,1)S(1)}, s32[]{:T(128)}, /*index=5*/s32[4]{0:T(128)S(1)}) while((s32[]{:T(128)}, bf16[2,32,16,1024]{3,2,0,1:T(8,128)(2,1)}, s32[2,4]{1,0:T(2,128)S(1)}, bf16[2,4,16,1024]{3,2,1,0:T(8,128)(2,1)S(1)}, s32[]{:T(128)}, ...), condition=%wide.while_cond, body=%wide.while_body.sunk | while | flops 65565 | bytes 657586 | solution.py:84
  190.7 3.3 %and_reduce_fusion.2 = pred[]{:T(512)} fusion(s32[4]{0:T(128)S(1)} %get-tuple-element.91, s32[1]{0:T(128)} %bitcast.71, s32[1]{0:T(128)} %bitcast.72, s32[1]{0:T(128)} %bitcast.73, s32[1]{0:T(128)} %bitcast.74), kind=kLoop, calls=%fused_computation.3.clone.1 | loop fusion | flops 27 | bytes 33 | tf_op jit(solution)/shard_map/vmap(vmap())/scatter
  194.0 2.2 constant_dynamic-slice_fusion.6
  196.2 2.6 bitcast_dynamic-update-slice_fusion.2
  198.8 0.7 fusion.24
  199.4 3.3 %and_reduce_fusion.2 = pred[]{:T(512)} fusion(s32[4]{0:T(128)S(1)} %get-tuple-element.91, s32[1]{0:T(128)} %bitcast.71, s32[1]{0:T(128)} %bitcast.72, s32[1]{0:T(128)} %bitcast.73, s32[1]{0:T(128)} %bitcast.74), kind=kLoop, calls=%fused_computation.3.clone.1 | loop fusion | flops 27 | bytes 33 | tf_op jit(solution)/shard_map/vmap(vmap())/scatter
  202.7 2.2 constant_dynamic-slice_fusion.6
  204.9 2.6 bitcast_dynamic-update-slice_fusion.2
  207.5 9.8 %all-to-all-start.1 = ((bf16[32,2,16,1024]{3,2,1,0:T(8,128)(2,1)}), bf16[32,2,16,1024]{3,2,1,0:T(8,128)(2,1)S(1)}, u32[]{:S(2)}, u32[]{:S(2)}) async-start(bf16[32,2,16,1024]{3,2,1,0:T(8,128)(2,1)} %bitcast.10), calls=%async_computation.2 | async-start | bytes 4194304 | tf_op jit(solution)/shard_map/all_to_all | solution.py:89
  217.3 7.5 %copy.33 = bf16[2,4,256,1024]{2,1,3,0:T(4,128)(2,1)} copy(bf16[2,4,256,1024]{3,2,1,0:T(8,128)(2,1)} %all-gather.6.cloned.1.call-done) | data formatting | bytes 8388608 | tf_op jit(solution)/shard_map/all_gather | solution.py:60
  224.8 7.7 %reshape_reshape.7 = bf16[2,1024,4,16,16]{1,4,3,2,0:T(8,128)(2,1)} reshape(bf16[2,4,256,1024]{2,1,3,0:T(4,128)(2,1)} %copy.33) | data formatting | bytes 8388608 | tf_op jit(solution)/shard_map/reshape;reshape | solution.py:67
  232.6 1.1 constant_dynamic-slice_fusion.2
  233.7 3.5 %convolution_multiply_fusion = f32[2,64,1024]{2,1,0:T(8,128)S(1)} fusion(bf16[2,1024,64]{1,2,0:T(8,128)(2,1)S(1)} %bitcast.84, bf16[2,1024,1024]{2,1,0:T(8,128)(2,1)} %bitcast.77), kind=kOutput, calls=%fused_computation.9 | convolution fusion | flops 268566528 | bytes 4980736 | tf_op jit(solution)/shard_map/mnr,mnc->mrc/dot_general | solution.py:73
  237.2 0.9 add.53
  238.1 1.4 convolution_multiply_fusion.1
  239.5 0.9 add.51
  240.3 27.4 %all-to-all-done.1 = bf16[32,2,16,1024]{3,2,1,0:T(8,128)(2,1)S(1)} async-done(((bf16[32,2,16,1024]{3,2,1,0:T(8,128)(2,1)}), bf16[32,2,16,1024]{3,2,1,0:T(8,128)(2,1)S(1)}, u32[]{:S(2)}, u32[]{:S(2)}) %all-to-all-start.1) | async-done | bytes 2097184 | tf_op jit(solution)/shard_map/all_to_all | solution.py:89
  267.7 1.2 fusion.5
  268.9 0.7 reshape.118
  (31 shorter events, 1.2 us)
Async XLA Ops:
  7.2 176.2 %copy-start = (bf16[2,4,1,16,1024]{4,3,2,1,0:T(8,128)(2,1)S(1)}, bf16[2,4,1,16,1024]{4,3,2,1,0:T(8,128)(2,1)}, u32[]{:S(2)}) copy-start(bf16[2,4,1,16,1024]{4,3,2,1,0:T(8,128)(2,1)} %param.10) | copy-start | bytes 786436
  7.2 71.7 %reduce-scatter.2.cloned.1.call-start = ((), (), s32[]{:S(2)}) async-start(), calls=%async_computation.3 | async-start | bytes 2228224 | tf_op jit(solution)/shard_map/reduce_scatter | solution.py:32
  7.9 132.7 %all-gather.4.cloned.1.call-start = ((), (), s32[]{:S(2)}) async-start(), calls=%async_computation.4 | async-start | bytes 4456448 | tf_op jit(solution)/shard_map/all_gather | solution.py:29
  80.7 12.4 %copy-start.7 = (s32[32]{0:T(128)S(1)}, s32[32]{0:T(128)}, u32[]{:S(2)}) copy-start(s32[32]{0:T(128)} %param.7) | copy-start | bytes 388
  80.7 59.7 %copy-start.6 = (s32[3]{0:T(128)S(1)}, s32[3]{0:T(128)}, u32[]{:S(2)}) copy-start(s32[3]{0:T(128)} %constant.55.clone.1) | copy-start | bytes 40
  83.2 55.9 %all-to-all-start = ((bf16[32,2,16,1024]{3,2,1,0:T(8,128)(2,1)}), bf16[32,2,16,1024]{3,2,1,0:T(8,128)(2,1)S(1)}, u32[]{:S(2)}, u32[]{:S(2)}) async-start(bf16[32,2,16,1024]{3,2,1,0:T(8,128)(2,1)} %bitcast.3), calls=%async_computation.1 | async-start | bytes 4194304 | tf_op jit(solution)/shard_map/all_to_all | solution.py:54
  93.1 90.3 %all-gather.6.cloned.1.call-start = ((), (), s32[]{:S(2)}) async-start(), calls=%async_computation.5 | async-start | bytes 4456448 | tf_op jit(solution)/shard_map/all_gather | solution.py:60
  183.4 6.7 %copy-start.5 = (s32[4]{0:T(128)S(1)}, s32[4]{0:T(128)}, u32[]{:S(2)}) copy-start(s32[4]{0:T(128)} %constant.139) | copy-start | bytes 52
  207.5 60.3 %all-to-all-start.1 = ((bf16[32,2,16,1024]{3,2,1,0:T(8,128)(2,1)}), bf16[32,2,16,1024]{3,2,1,0:T(8,128)(2,1)S(1)}, u32[]{:S(2)}, u32[]{:S(2)}) async-start(bf16[32,2,16,1024]{3,2,1,0:T(8,128)(2,1)} %bitcast.10), calls=%async_computation.2 | async-start | bytes 4194304 | tf_op jit(solution)/shard_map/all_to_all | solution.py:89
  232.6 4.6 %copy-start.3 = (f32[2,4,1,16,1024]{4,3,2,1,0:T(8,128)S(1)}, f32[2,4,1,16,1024]{4,3,2,1,0:T(8,128)}, u32[]{:S(2)}) copy-start(f32[2,4,1,16,1024]{4,3,2,1,0:T(8,128)} %param.9) | copy-start | bytes 1572868
  232.6 5.5 %copy-start.1 = (bf16[2,4,256,1024]{3,2,1,0:T(8,128)(2,1)S(1)}, bf16[2,4,256,1024]{3,2,1,0:T(8,128)(2,1)}, u32[]{:S(2)}) copy-start(bf16[2,4,256,1024]{3,2,1,0:T(8,128)(2,1)} %all-gather.6.cloned.1.call-done) | copy-start | bytes 12582916
  232.6 5.5 %copy-start.2 = (bf16[2,4,16,1024]{3,2,1,0:T(8,128)(2,1)S(1)}, bf16[2,4,16,1024]{3,2,1,0:T(8,128)(2,1)}, u32[]{:S(2)}) copy-start(bf16[2,4,16,1024]{3,2,1,0:T(8,128)(2,1)} %gather_fusion) | copy-start | bytes 786436
  237.2 2.3 copy-start.4
Sparse Core Ops, SparseCore 0:
  10.8 68.0 reduce-scatter.1
  81.0 42.9 all-gather.3
  140.6 42.7 all-gather.5
where the time goes:
time: 277 us; the launch traced here: 276 us
  waiting for transfers between devices  187 us (68%)
  local copies, waits for them, and re-layouts  30.1 us (11%)
  starting transfers between devices  19.8 us (7%)
  between operations  13.9 us (5%)
  other arithmetic  13.7 us (5%)
  matrix products  12 us (4%)
    reduce_scatter x1, waiting for transfers between devices, on_device(): lax.psum_scatter(replica_grads[0].astype(jnp.float32).astype(jnp.bfloat16...  69.5 us
    all_to_all x1, waiting for transfers between devices, on_device(): lax.all_to_all(outgoing, 'fsdp', split_axis=0, concat_axis=0, tiled=True)  45.8 us
    all_gather x1, waiting for transfers between devices, on_device(): lax.all_gather(owned_rows, 'dp', axis=2, tiled=True)  42.7 us
    all_to_all x1, waiting for transfers between devices, on_device(): lax.all_to_all(homeward, 'fsdp', split_axis=0, concat_axis=0, tiled=True)  27.4 us
    scatter x4, other arithmetic  11.7 us
    all_to_all x1, starting transfers between devices, on_device(): lax.all_to_all(outgoing, 'fsdp', split_axis=0, concat_axis=0, tiled=True)  9.83 us
    all_to_all x1, starting transfers between devices, on_device(): lax.all_to_all(homeward, 'fsdp', split_axis=0, concat_axis=0, tiled=True)  9.82 us
    another operation x1, local copies, waits for them, and re-layouts, on_device(): entire.reshape(slots_here, block_size, sub_blocks, groups, strip_rows)  7.75 us
  transfers between devices with their start and end apart: 5, of which 4 were waited for; matrix products, arithmetic and copies ran while one was open for 11% of the time, Pallas kernels for 0%

commit v1 on v0

--- a/solution.py
+++ b/solution.py
@@ -57,7 +57,7 @@
         in_axes=(1, 0),
     )(arrived, first_band)
     owned_rows = owned_rows.reshape(slots_here, sub_blocks, 1, strip_rows, block_size)
-    entire = lax.all_gather(owned_rows, "dp", axis=2, tiled=True).reshape(
+    entire = jnp.concatenate(lax.all_gather(owned_rows, "dp"), axis=2).reshape(
         slots_here, block_size, block_size
     )
     my_rows = owned_rows.reshape(slots_here, sub_blocks * strip_rows, block_size)

time: 277 us -> 329 us (1.19)
  the two profiles are of different devices: /device:TPU:16 before, /device:TPU:1 now
where the time goes in v1:
time: 329 us; the launch traced here: 327 us
  waiting for transfers between devices  202 us (61%)
  local copies, waits for them, and re-layouts  68.1 us (21%)
  starting transfers between devices  18.2 us (6%)
  between operations  13.9 us (4%)
  other arithmetic  13.6 us (4%)
  matrix products  11.7 us (4%)
    reduce_scatter x1, waiting for transfers between devices, on_device(): lax.psum_scatter(replica_grads[0].astype(jnp.float32).astype(jnp.bfloat16...  68.4 us
    all_gather x1, waiting for transfers between devices, on_device(): lax.all_gather(owned_rows, 'dp')  45.9 us
    all_to_all x1, waiting for transfers between devices, on_device(): lax.all_to_all(outgoing, 'fsdp', split_axis=0, concat_axis=0, tiled=True)  45.8 us
    all_gather x1, waiting for transfers between devices, on_device(): lax.all_gather(right_inverse_root, 'dp', axis=2, tiled=True)  40.3 us
    another operation x1, local copies, waits for them, and re-layouts, on_device(): entire.reshape(slots_here, block_size, sub_blocks, groups, strip_rows)  31.7 us
    dynamic_slice x2, local copies, waits for them, and re-layouts, on_device(): lax.dynamic_index_in_dim(entire.reshape(slots_here, block_size, sub_block...  17.7 us
    scatter x4, other arithmetic  11.6 us
    all_to_all x1, starting transfers between devices, on_device(): lax.all_to_all(outgoing, 'fsdp', split_axis=0, concat_axis=0, tiled=True)  9.06 us
  transfers between devices with their start and end apart: 5, of which 4 were waited for; matrix products, arithmetic and copies ran while one was open for 19% of the time, Pallas kernels for 0%

profile of v1, /device:TPU:1, one launch (start us, length us, event | category | flops | bytes accessed | tf_op | source)
XLA Modules:
  0.0 327.3 jit_solution(9164719099686930624)
XLA Ops:
  7.2 0.7 reduce-scatter.2.cloned.1.call-update
  7.9 0.7 dynamic_slice.7
  8.7 68.4 %reduce-scatter.2.cloned.1.call-done = bf16[16,4096]{1,0:T(8,128)(2,1)} async-done(((bf16[256,4096]{1,0:T(8,128)(2,1)}), bf16[16,4096]{1,0:T(8,128)(2,1)}) %reduce-scatter.2.cloned.1.call-update) | async-done | bytes 131088 | tf_op jit(solution)/shard_map/reduce_scatter | solution.py:32
  77.1 1.0 reshape.107
  78.1 0.8 convolution_convert_fusion
  78.9 2.5 copy.39
  81.4 9.1 %all-to-all-start = ((bf16[32,2,16,1024]{3,2,1,0:T(8,128)(2,1)}), bf16[32,2,16,1024]{3,2,1,0:T(8,128)(2,1)S(1)}, u32[]{:S(2)}, u32[]{:S(2)}) async-start(bf16[32,2,16,1024]{3,2,1,0:T(8,128)(2,1)} %bitcast.3), calls=%async_computation.1 | async-start | bytes 4194304 | tf_op jit(solution)/shard_map/all_to_all | solution.py:54
  90.8 45.8 %all-to-all-done = bf16[32,2,16,1024]{3,2,1,0:T(8,128)(2,1)S(1)} async-done(((bf16[32,2,16,1024]{3,2,1,0:T(8,128)(2,1)}), bf16[32,2,16,1024]{3,2,1,0:T(8,128)(2,1)S(1)}, u32[]{:S(2)}, u32[]{:S(2)}) %all-to-all-start) | async-done | bytes 2097184 | tf_op jit(solution)/shard_map/all_to_all | solution.py:54
  136.6 1.3 gather_fusion
  137.9 0.7 all-gather.4.cloned.1.call-update
  138.8 45.9 %all-gather.6.cloned.1.call-done = bf16[32,4,16,1024]{3,2,1,0:T(8,128)(2,1)} async-done(((bf16[2,4,16,1024]{3,2,1,0:T(8,128)(2,1)}), bf16[32,4,16,1024]{3,2,1,0:T(8,128)(2,1)}) %all-gather.6.cloned.1.call-update) | async-done | bytes 4194320 | tf_op jit(solution)/shard_map/all_gather | solution.py:60
  184.7 5.1 %copy.52 = bf16[16,2,4,1,16,1024]{5,4,0,2,1,3:T(8,128)(2,1)} copy(bf16[16,2,4,1,16,1024]{5,4,2,1,0,3:T(8,128)(2,1)} %bitcast.88) | data formatting | bytes 8388608 | tf_op jit(solution)/shard_map/all_gather | solution.py:60
  189.8 40.3 %all-gather.4.cloned.1.call-done = bf16[2,4,16,16,1024]{4,3,2,1,0:T(8,128)(2,1)} async-done(((bf16[2,4,1,16,1024]{4,3,2,1,0:T(8,128)(2,1)}), bf16[2,4,16,16,1024]{4,3,2,1,0:T(8,128)(2,1)}) %all-gather.4.cloned.1.call-update) | async-done | bytes 4194320 | tf_op jit(solution)/shard_map/all_gather | solution.py:29
  230.1 5.1 %convolution_convert_fusion.2 = bf16[2,64,1024]{2,1,0:T(8,128)(2,1)S(1)} fusion(bf16[2,1024,1024]{2,1,0:T(8,128)(2,1)} %bitcast.89, bf16[2,64,1024]{2,1,0:T(8,128)(2,1)S(1)} %bitcast.82, bf16[2,1024,1024]{2,1,0:T(8,128)(2,1)} %bitcast.83), kind=kOutput, calls=%fused_computation.12 | convolution fusion | flops 537133056 | bytes 8912896 | tf_op jit(solution)/shard_map/mrn,mnc->mrc/dot_general | solution.py:79
  235.2 1.6 broadcast_in_dim.16.clone
  236.8 17.2 %while.1 = (s32[]{:T(128)}, bf16[2,32,16,1024]{3,2,0,1:T(8,128)(2,1)}, s32[2,4]{1,0:T(2,128)S(1)}, bf16[2,4,16,1024]{3,2,1,0:T(8,128)(2,1)S(1)}, s32[]{:T(128)}, /*index=5*/s32[4]{0:T(128)S(1)}) while((s32[]{:T(128)}, bf16[2,32,16,1024]{3,2,0,1:T(8,128)(2,1)}, s32[2,4]{1,0:T(2,128)S(1)}, bf16[2,4,16,1024]{3,2,1,0:T(8,128)(2,1)S(1)}, s32[]{:T(128)}, ...), condition=%wide.while_cond, body=%wide.while_body.sunk | while | flops 65565 | bytes 657586 | solution.py:84
  237.5 3.3 and_reduce_fusion.2
  240.8 2.1 constant_dynamic-slice_fusion.6
  242.9 2.5 bitcast_dynamic-update-slice_fusion.2
  246.1 3.3 and_reduce_fusion.2
  249.3 2.1 constant_dynamic-slice_fusion.6
  251.5 2.5 bitcast_dynamic-update-slice_fusion.2
  254.0 9.0 %all-to-all-start.1 = ((bf16[32,2,16,1024]{3,2,1,0:T(8,128)(2,1)}), bf16[32,2,16,1024]{3,2,1,0:T(8,128)(2,1)S(1)}, u32[]{:S(2)}, u32[]{:S(2)}) async-start(bf16[32,2,16,1024]{3,2,1,0:T(8,128)(2,1)} %bitcast.12), calls=%async_computation.2 | async-start | bytes 4194304 | tf_op jit(solution)/shard_map/all_to_all | solution.py:89
  263.1 31.7 %reshape_reshape_reshape.3 = bf16[2,1024,4,16,16]{4,3,2,1,0:T(8,128)(2,1)} reshape(bf16[2,4,16,1,16,1024]{5,4,2,1,0,3:T(8,128)(2,1)} %bitcast.84) | data formatting | bytes 8388608 | tf_op jit(solution)/shard_map/reshape;reshape;reshape | solution.py:67
  294.8 9.0 %constant_dynamic-slice_fusion.2 = bf16[2,1024,4,1,16]{4,3,2,1,0:T(2,128)(2,1)} fusion(bf16[2,1024,4,16,16]{4,3,2,1,0:T(8,128)(2,1)} %reshape_reshape_reshape.3, s32[]{:T(128)S(6)} %select_n.44), kind=kLoop, calls=%fused_computation.31 | loop fusion | bytes 524292 | tf_op jit(solution)/shard_map/jit(dynamic_index_in_dim)/dynamic_slice | solution.py:66
  303.8 8.7 %copy.37 = bf16[2,1024,4,1,16]{1,4,2,0,3:T(8,128)(2,1)S(1)} copy(bf16[2,1024,4,1,16]{4,3,2,1,0:T(2,128)(2,1)} %constant_dynamic-slice_fusion.2) | data formatting | bytes 524288 | tf_op jit(solution)/shard_map/jit(dynamic_index_in_dim)/dynamic_slice | solution.py:66
  312.5 3.2 convolution_multiply_fusion
  315.7 0.9 add.53
  316.6 1.4 convolution_multiply_fusion.1
  318.0 0.9 add.51
  318.8 1.2 fusion.5
  320.1 0.7 reshape.114
  (34 shorter events, 1.9 us)
Async XLA Ops:
  7.2 223.0 %copy-start = (bf16[2,4,1,16,1024]{4,3,2,1,0:T(8,128)(2,1)S(1)}, bf16[2,4,1,16,1024]{4,3,2,1,0:T(8,128)(2,1)}, u32[]{:S(2)}) copy-start(bf16[2,4,1,16,1024]{4,3,2,1,0:T(8,128)(2,1)} %param.10) | copy-start | bytes 786436
  7.2 69.9 %reduce-scatter.2.cloned.1.call-start = ((), (), s32[]{:S(2)}) async-start(), calls=%async_computation.3 | async-start | bytes 2228224 | tf_op jit(solution)/shard_map/reduce_scatter | solution.py:32
  78.9 11.6 %copy-start.8 = (s32[32]{0:T(128)S(1)}, s32[32]{0:T(128)}, u32[]{:S(2)}) copy-start(s32[32]{0:T(128)} %param.7) | copy-start | bytes 388
  78.9 59.7 %copy-start.7 = (s32[3]{0:T(128)S(1)}, s32[3]{0:T(128)}, u32[]{:S(2)}) copy-start(s32[3]{0:T(128)} %constant.55.clone.1) | copy-start | bytes 40
  81.4 55.2 %all-to-all-start = ((bf16[32,2,16,1024]{3,2,1,0:T(8,128)(2,1)}), bf16[32,2,16,1024]{3,2,1,0:T(8,128)(2,1)S(1)}, u32[]{:S(2)}, u32[]{:S(2)}) async-start(bf16[32,2,16,1024]{3,2,1,0:T(8,128)(2,1)} %bitcast.3), calls=%async_computation.1 | async-start | bytes 4194304 | tf_op jit(solution)/shard_map/all_to_all | solution.py:54
  90.5 94.3 %all-gather.6.cloned.1.call-start = ((), (), s32[]{:S(2)}) async-start(), calls=%async_computation.5 | async-start | bytes 4456448 | tf_op jit(solution)/shard_map/all_gather | solution.py:60
  137.9 92.2 %all-gather.4.cloned.1.call-start = ((), (), s32[]{:S(2)}) async-start(), calls=%async_computation.4 | async-start | bytes 4456448 | tf_op jit(solution)/shard_map/all_gather | solution.py:29
  230.1 6.7 %copy-start.6 = (s32[4]{0:T(128)S(1)}, s32[4]{0:T(128)}, u32[]{:S(2)}) copy-start(s32[4]{0:T(128)} %constant.139) | copy-start | bytes 52
  254.0 64.8 %all-to-all-start.1 = ((bf16[32,2,16,1024]{3,2,1,0:T(8,128)(2,1)}), bf16[32,2,16,1024]{3,2,1,0:T(8,128)(2,1)S(1)}, u32[]{:S(2)}, u32[]{:S(2)}) async-start(bf16[32,2,16,1024]{3,2,1,0:T(8,128)(2,1)} %bitcast.12), calls=%async_computation.2 | async-start | bytes 4194304 | tf_op jit(solution)/shard_map/all_to_all | solution.py:89
  303.8 11.9 %copy-start.4 = (f32[2,4,1,16,1024]{4,3,2,1,0:T(8,128)S(1)}, f32[2,4,1,16,1024]{4,3,2,1,0:T(8,128)}, u32[]{:S(2)}) copy-start(f32[2,4,1,16,1024]{4,3,2,1,0:T(8,128)} %param.9) | copy-start | bytes 1572868
  312.5 4.1 %copy-start.2 = (bf16[16,2,4,1,16,1024]{5,4,0,2,1,3:T(8,128)(2,1)S(1)}, bf16[16,2,4,1,16,1024]{5,4,0,2,1,3:T(8,128)(2,1)}, u32[]{:S(2)}) copy-start(bf16[16,2,4,1,16,1024]{5,4,0,2,1,3:T(8,128)(2,1)} %copy.52) | copy-start | bytes 12582916
  312.5 4.1 %copy-start.3 = (bf16[2,4,16,1024]{3,2,1,0:T(8,128)(2,1)S(1)}, bf16[2,4,16,1024]{3,2,1,0:T(8,128)(2,1)}, u32[]{:S(2)}) copy-start(bf16[2,4,16,1024]{3,2,1,0:T(8,128)(2,1)} %gather_fusion) | copy-start | bytes 786436
  315.7 2.3 copy-start.5
  316.6 4.2 %copy-start.1 = (bf16[2,4,1,16,1024]{4,3,2,1,0:T(8,128)(2,1)S(1)}, bf16[2,4,1,16,1024]{4,3,2,1,0:T(8,128)(2,1)}, u32[]{:S(2)}) copy-start(bf16[2,4,1,16,1024]{4,3,2,1,0:T(8,128)(2,1)} %param.10) | copy-start | bytes 786436
Sparse Core Ops, SparseCore 0:
  10.8 66.2 reduce-scatter.1
  138.0 46.6 all-gather.5
  186.9 43.2 all-gather.3
